TPU v7x, 32 devices: a whole 2x2x4 slice. The times are simulated.
32 devices in a mesh: dp: 8 (over z, y), mp: 2 (over core), fsdp: 2 (over x).
Axes of the slice: x: 2, y: 2, z: 4, core: 2. Of those that a mesh axis runs over, the one named last changes fastest.
Arguments:
- features: bfloat16 [5, 1024, 512], P(None, ('dp', 'fsdp')), may hold values from -6 to 6
- memory_bank: bfloat16 [512, 32, 1024], P(('dp', 'fsdp')), may hold values from -1 to 1
- memory_fill: int32 [512], P(('dp', 'fsdp')), may hold values from 0 to 32
- left_keys: bfloat16 [512, 64, 1024], P(('dp', 'fsdp'), None, 'mp'), may hold values from -400 to 400
- left_values: bfloat16 [512, 64, 1024], P(('dp', 'fsdp'), None, 'mp'), may hold values from -6 to 6
- left_length: int32 [512], P(('dp', 'fsdp')), may hold values from 0 to 64
- w_query: bfloat16 [1024, 1024], P('fsdp', 'mp'), may hold values from -0.1875 to 0.1875
- w_key: bfloat16 [1024, 1024], P('fsdp', 'mp'), may hold values from -0.1875 to 0.1875
- w_value: bfloat16 [1024, 1024], P('fsdp', 'mp'), may hold values from -0.1875 to 0.1875
- w_out: bfloat16 [1024, 1024], P('mp', 'fsdp'), may hold values from -0.1875 to 0.1875
- w_up: bfloat16 [1024, 4096], P('fsdp', 'mp'), may hold values from -0.1875 to 0.1875
- w_down: bfloat16 [4096, 1024], P('mp', 'fsdp'), may hold values from -0.09375 to 0.09375
- out_gain: float32 [1024], replicated, may hold values from 0.1 to 1.9
Outputs:
- layer_out: bfloat16 [512, 5, 1024], P(('dp', 'fsdp'))
- memory_next: bfloat16 [512, 1024], P(('dp', 'fsdp'))
- center_keys: bfloat16 [512, 4, 1024], P(('dp', 'fsdp'), None, 'mp')
- center_values: bfloat16 [512, 4, 1024], P(('dp', 'fsdp'), None, 'mp')
All inputs are finite; a program needn't handle non-finite values.
Results may differ from a plain program's by a relative error of at most 0.0095.
Values may be sent and summed in bfloat16 or wider, within the bound.
A program may use at most 128 MiB of HBM per device.

v0:
```python
import jax
import jax.numpy as jnp
from jax import lax
from jax.sharding import PartitionSpec as P

HD = 64
GROUP = 4
epsilon = 1e-05
masked_score = -1e30


def normalize(values):
    values = values.astype(jnp.float32)
    average = jnp.mean(values, axis=-1, keepdims=True)
    centred = values - average
    variance = jnp.mean(centred * centred, axis=-1, keepdims=True)
    return centred * lax.rsqrt(variance + epsilon)


def matmul(left, right):
    return jnp.dot(left, right, preferred_element_type=jnp.float32)


def shards(
    features,
    memory_bank,
    memory_fill,
    left_keys,
    left_values,
    left_length,
    w_query,
    w_key,
    w_value,
    w_out,
    w_up,
    w_down,
    out_gain,
):
    frames, width_dev, all_streams = features.shape
    streams, mem_slots, width = memory_bank.shape
    left_slots = left_keys.shape[1]
    head_cols = w_query.shape[1]
    head_count = head_cols // HD
    flattened = features.reshape(frames * width_dev, all_streams)
    n_dp = lax.axis_size("dp")
    n_fsdp = lax.axis_size("fsdp")
    arrived = lax.all_to_all(flattened, ("dp", "fsdp"), split_axis=1, concat_axis=0, tiled=True)
    arrived = arrived.reshape(n_dp * n_fsdp, frames, width_dev, streams)
    inputs = jnp.transpose(arrived, (3, 1, 0, 2)).reshape(streams, frames, width)
    normed = normalize(inputs).astype(jnp.bfloat16)
    summary = jnp.mean(normed[:, :GROUP, :].astype(jnp.float32), axis=1).astype(jnp.bfloat16)
    query_rows = jnp.concatenate([normed, summary[:, None, :]], axis=1).reshape(-1, width)
    key_rows = jnp.concatenate([normed.reshape(-1, width), memory_bank.reshape(-1, width)], axis=0)
    query_sums = matmul(query_rows, lax.all_gather(w_query, "fsdp", axis=0, tiled=True))
    key_sums = matmul(key_rows, lax.all_gather(w_key, "fsdp", axis=0, tiled=True))
    value_sums = matmul(key_rows, lax.all_gather(w_value, "fsdp", axis=0, tiled=True))
    query_proj = query_sums.astype(jnp.bfloat16)
    key_proj = key_sums.astype(jnp.bfloat16)
    value_proj = value_sums.astype(jnp.bfloat16)
    group_total = streams * frames
    query_h = query_proj.reshape(streams, frames + 1, head_count, HD)
    ckey_h = key_proj[:group_total].reshape(streams, frames, head_count, HD)
    cval_h = value_proj[:group_total].reshape(streams, frames, head_count, HD)
    mkey_h = key_proj[group_total:].reshape(streams, mem_slots, head_count, HD)
    mval_h = value_proj[group_total:].reshape(streams, mem_slots, head_count, HD)
    lkey_h = left_keys.reshape(streams, left_slots, head_count, HD)
    lval_h = left_values.reshape(streams, left_slots, head_count, HD)
    not_summary = jnp.arange(frames + 1, dtype=jnp.int32) < frames
    mem_ok = jnp.arange(mem_slots, dtype=jnp.int32)[None, :] >= (mem_slots - memory_fill)[:, None]
    mem_mask = mem_ok[:, None, None, :] & not_summary[None, None, :, None]
    left_ok = (
        jnp.arange(left_slots, dtype=jnp.int32)[None, :] >= (left_slots - left_length)[:, None]
    )
    left_mask = left_ok[:, None, None, :]
    scale = HD ** (-0.5)
    score_mem = (
        jnp.einsum("sqhd,skhd->shqk", query_h, mkey_h, preferred_element_type=jnp.float32) * scale
    )
    score_left = (
        jnp.einsum("sqhd,skhd->shqk", query_h, lkey_h, preferred_element_type=jnp.float32) * scale
    )
    score_group = (
        jnp.einsum("sqhd,skhd->shqk", query_h, ckey_h, preferred_element_type=jnp.float32) * scale
    )
    score_mem = jnp.where(mem_mask, score_mem, masked_score)
    score_left = jnp.where(left_mask, score_left, masked_score)
    top = jnp.maximum(
        jnp.maximum(
            jnp.max(score_mem, axis=-1, keepdims=True), jnp.max(score_left, axis=-1, keepdims=True)
        ),
        jnp.max(score_group, axis=-1, keepdims=True),
    )
    exp_mem = jnp.exp(score_mem - top)
    exp_left = jnp.exp(score_left - top)
    exp_group = jnp.exp(score_group - top)
    totals = (
        jnp.sum(exp_mem, axis=-1, keepdims=True)
        + jnp.sum(exp_left, axis=-1, keepdims=True)
        + jnp.sum(exp_group, axis=-1, keepdims=True)
    )
    prob_mem = (exp_mem / totals).astype(jnp.bfloat16)
    prob_left = (exp_left / totals).astype(jnp.bfloat16)
    prob_group = (exp_group / totals).astype(jnp.bfloat16)
    attended = jnp.einsum("shqk,skhd->sqhd", prob_mem, mval_h, preferred_element_type=jnp.float32)
    attended = attended + jnp.einsum(
        "shqk,skhd->sqhd", prob_left, lval_h, preferred_element_type=jnp.float32
    )
    attended = attended + jnp.einsum(
        "shqk,skhd->sqhd", prob_group, cval_h, preferred_element_type=jnp.float32
    )
    attended = attended.astype(jnp.bfloat16).reshape(streams * (frames + 1), head_cols)
    attn_part = matmul(attended, lax.all_gather(w_out, "fsdp", axis=1, tiled=True))
    attn_out = (
        lax.psum(attn_part.astype(jnp.bfloat16), "mp")
        .astype(jnp.float32)
        .reshape(streams, frames + 1, width)
    )
    memory_next = jnp.tanh(attn_out[:, frames, :]).astype(jnp.bfloat16)
    hidden_state = inputs.astype(jnp.float32) + attn_out[:, :frames, :]
    h_norm = normalize(hidden_state).astype(jnp.bfloat16).reshape(-1, width)
    halves = lax.all_to_all(h_norm, "fsdp", split_axis=1, concat_axis=0, tiled=True)
    up_sums = lax.psum_scatter(
        matmul(halves, w_up).astype(jnp.bfloat16), "fsdp", scatter_dimension=0, tiled=True
    ).astype(jnp.float32)
    hidden = jax.nn.gelu(up_sums, approximate=True).astype(jnp.bfloat16)
    down_all = matmul(lax.all_gather(hidden, "fsdp", axis=0, tiled=True), w_down)
    down_part = lax.all_to_all(
        down_all.astype(jnp.bfloat16), "fsdp", split_axis=0, concat_axis=1, tiled=True
    ).astype(down_all.dtype)
    down_proj = lax.psum(down_part.astype(jnp.bfloat16), "mp").astype(jnp.float32)
    layer_out = (
        (normalize(hidden_state.reshape(-1, width) + down_proj) * out_gain)
        .astype(jnp.bfloat16)
        .reshape(streams, frames, width)
    )
    center_keys = key_proj[:group_total].reshape(streams, frames, head_cols)[:, :GROUP, :]
    center_values = value_proj[:group_total].reshape(streams, frames, head_cols)[:, :GROUP, :]
    return (layer_out, memory_next, center_keys, center_values)


def solution(mesh):
    in_specs = (
        P(None, ("dp", "fsdp"), None),
        P(("dp", "fsdp"), None, None),
        P(("dp", "fsdp")),
        P(("dp", "fsdp"), None, "mp"),
        P(("dp", "fsdp"), None, "mp"),
        P(("dp", "fsdp")),
        P("fsdp", "mp"),
        P("fsdp", "mp"),
        P("fsdp", "mp"),
        P("mp", "fsdp"),
        P("fsdp", "mp"),
        P("mp", "fsdp"),
        P(),
    )
    out_specs = (
        P(("dp", "fsdp"), None, None),
        P(("dp", "fsdp"), None),
        P(("dp", "fsdp"), None, "mp"),
        P(("dp", "fsdp"), None, "mp"),
    )
    return jax.shard_map(shards, mesh=mesh, in_specs=in_specs, out_specs=out_specs, check_vma=False)
```

profile of v0, /device:TPU:0, one launch (start us, length us, event | category | flops | bytes accessed | tf_op | source)
XLA Modules:
  0.0 236.4 jit_solution(17857175718315085044)
XLA Ops:
  7.2 0.7 all-gather.10.cloned.1.call-update
  8.0 0.7 all-gather.8.cloned.1.call-update
  8.7 0.7 all-gather.6.cloned.1.call-update
  9.4 1.8 copy.120
  11.2 1.4 all_to_all.38
  12.6 8.3 %all-to-all-start = ((bf16[320,16,32]{0,2,1:T(8,128)(2,1)}), bf16[320,16,32]{0,2,1:T(8,128)(2,1)S(1)}, u32[]{:S(2)}, u32[]{:S(2)}) async-start(bf16[320,16,32]{0,2,1:T(8,128)(2,1)} %all_to_all.38), calls=%async_computation | async-start | bytes 786432 | tf_op jit(solution)/shard_map/all_to_all | solution.py:47
  21.6 6.2 %reshape.219 = bf16[32,64,8,64]{3,2,1,0:T(8,128)(2,1)} reshape(bf16[32,64,512]{2,1,0:T(8,128)(2,1)} %param.16) | data formatting | bytes 4194304 | tf_op jit(solution)/shard_map/reshape | solution.py:66
  27.8 6.2 %reshape.221 = bf16[32,64,8,64]{3,2,1,0:T(8,128)(2,1)} reshape(bf16[32,64,512]{2,1,0:T(8,128)(2,1)} %param.17) | data formatting | bytes 4194304 | tf_op jit(solution)/shard_map/reshape | solution.py:67
  34.2 1.7 reshape.233
  35.9 1.8 bitcast_reduce_fusion
  37.9 2.1 multiply_reduce_fusion
  40.1 3.6 %copy.121 = f32[32,5,16,64]{3,2,0,1:T(8,128)} copy(f32[32,5,16,64]{3,1,0,2:T(8,128)} %bitcast.51) | data formatting | bytes 1310720 | tf_op jit(solution)/shard_map/convert_element_type | solution.py:119
  43.7 1.9 copy.122
  45.7 1.8 reshape.230
  48.0 0.9 reshape.216
  49.0 1.7 reshape.231
  50.7 0.9 multiply_convert_fusion.3
  51.6 3.4 %convolution_convert_fusion = bf16[1184,512]{1,0:T(8,128)(2,1)S(1)} fusion(bf16[1024,512]{1,0:T(8,128)(2,1)} %all-gather.10.cloned.1.call-done, bf16[1024,1024]{1,0:T(8,128)(2,1)} %bitcast.57, bf16[160,1024]{1,0:T(8,128)(2,1)} %multiply_convert_fusion.3), kind=kOutput, calls=%fused_computation.4 | convolution fusion | flops 1246969856 | bytes 4685824 | tf_op jit(solution)/shard_map/dot_general | solution.py:21
  55.0 0.7 slice.41
  55.7 1.0 slice.40
  56.7 3.9 %all-gather.8.cloned.1.call-done = bf16[1024,512]{1,0:T(8,128)(2,1)} async-done(((bf16[512,512]{1,0:T(8,128)(2,1)}), bf16[1024,512]{1,0:T(8,128)(2,1)}) %all-gather.8.cloned.1.call-update) | async-done | bytes 1048592 | tf_op jit(solution)/shard_map/all_gather | solution.py:54
  60.6 1.6 convolution_convert_fusion.5
  62.5 1.1 reshape.220
  63.6 3.9 %reshape.218 = bf16[32,32,8,64]{3,2,1,0:T(8,128)(2,1)} reshape(bf16[1024,512]{1,0:T(8,128)(2,1)} %slice.40) | data formatting | bytes 2097152 | tf_op jit(solution)/shard_map/reshape | solution.py:64
  68.1 3.8 %fusion.63 = (f32[32,8,6]{2,1,0:T(8,128)S(1)}, f32[32,8,6,32]{3,2,1,0:T(8,128)S(1)}) fusion(bf16[32,32,8,64]{3,2,1,0:T(8,128)(2,1)} %reshape.218, bf16[32,6,8,64]{3,2,1,0:T(8,128)(2,1)S(1)} %reshape.217, pred[32,6,32]{2,1,0:T(8,128)(4,1)S(1)} %broadcast_and_fusion), kind=kOutput, calls=%fused_computation.93 | convolution fusion | flops 6437376 | bytes 1454080 | tf_op jit(solution)/shard_map/sqhd,skhd->shqk/dot_general | solution.py:77
  71.8 2.4 fusion.64
  74.2 1.0 copy-done.3
  77.0 6.5 %all-gather.6.cloned.1.call-done = bf16[1024,512]{1,0:T(8,128)(2,1)} async-done(((bf16[512,512]{1,0:T(8,128)(2,1)}), bf16[1024,512]{1,0:T(8,128)(2,1)}) %all-gather.6.cloned.1.call-update) | async-done | bytes 1048592 | tf_op jit(solution)/shard_map/all_gather | solution.py:56
  83.5 3.4 %convolution_convert_fusion.1 = bf16[1184,512]{1,0:T(8,128)(2,1)S(1)} fusion(bf16[1024,512]{1,0:T(8,128)(2,1)} %all-gather.6.cloned.1.call-done, bf16[1024,1024]{1,0:T(8,128)(2,1)} %bitcast.58, bf16[160,1024]{1,0:T(8,128)(2,1)} %multiply_convert_fusion.3), kind=kOutput, calls=%fused_computation.5 | convolution fusion | flops 1246969856 | bytes 4685824 | tf_op jit(solution)/shard_map/dot_general | solution.py:21
  86.9 1.0 copy-done.14
  87.9 0.9 reshape.222
  88.9 3.0 %convolution_bitcast_fusion = f32[32,6,8,64]{3,1,2,0:T(8,128)} fusion(f32[32,8,6,5]{2,3,1,0:T(8,128)} %copy-done.6, bf16[32,5,8,64]{3,2,1,0:T(8,128)(2,1)} %reshape.222, f32[32,8,6]{2,1,0:T(8,128)S(1)} %add_add_fusion, f32[32,8,6]{2,1,0:T(8,128)S(1)} %maximum_maximum_fusion), kind=kOutput, calls=%fused_computation.23 | convolution fusion | flops 1006080 | bytes 600064 | tf_op jit(solution)/shard_map/shqk,skhd->sqhd/dot_general | solution.py:108
  91.9 1.0 slice.38
  93.0 3.9 %reshape.215 = bf16[32,32,8,64]{3,2,1,0:T(8,128)(2,1)} reshape(bf16[1024,512]{1,0:T(8,128)(2,1)} %slice.38) | data formatting | bytes 2097152 | tf_op jit(solution)/shard_map/reshape | solution.py:65
  96.9 2.7 %fusion.8 = f32[32,6,8,64]{3,1,2,0:T(8,128)S(1)} fusion(bf16[32,32,8,64]{3,2,1,0:T(8,128)(2,1)} %reshape.215, f32[32,8,6,32]{3,2,1,0:T(8,128)} %copy-done.7, f32[32,8,6]{2,1,0:T(8,128)S(1)} %copy-done.17, f32[32,8,6]{2,1,0:T(8,128)S(1)} %maximum_maximum_fusion), kind=kOutput, calls=%fused_computation.17 | convolution fusion | flops 6438912 | bytes 1650688 | tf_op jit(solution)/shard_map/shqk,skhd->sqhd/dot_general | solution.py:104
  99.7 0.7 copy-done.5
  100.6 1.5 fusion.38
  102.4 3.8 %all-gather.12.cloned.1.call-done = bf16[512,1024]{1,0:T(8,128)(2,1)} async-done(((bf16[512,512]{1,0:T(8,128)(2,1)}), bf16[512,1024]{1,0:T(8,128)(2,1)}) %all-gather.12.cloned.1.call-update) | async-done | bytes 1048592 | tf_op jit(solution)/shard_map/all_gather | solution.py:112
  106.2 2.4 convolution_convert_fusion.3
  108.6 1.1 reshape.224
  109.7 1.0 copy.140
  110.8 18.5 %all-reduce.3.cloned.1.call-done = bf16[32,6,1024]{2,0,1:T(8,128)(2,1)} async-done(((bf16[32,6,1024]{2,0,1:T(8,128)(2,1)}), bf16[32,6,1024]{2,0,1:T(8,128)(2,1)}) %all-reduce.3.cloned.1.call-update) | async-done | bytes 393232 | tf_op jit(solution)/shard_map/psum | solution.py:114
  129.3 1.1 reshape.225
  130.5 0.7 copy-done.8
  131.8 1.0 all_to_all.40
  132.8 1.0 copy.143
  133.8 9.1 %all_to_all.51 = bf16[160,2,512]{2,0,1:T(8,128)(2,1)S(1)} all-to-all(bf16[160,2,512]{2,0,1:T(8,128)(2,1)S(1)} %copy.143), channel_id=1, replica_groups=mesh['dp'=8,'mp'=2,'fsdp'=2] {'fsdp'}, dimensions={1} | all-to-all | bytes 655360 | tf_op jit(solution)/shard_map/all_to_all | solution.py:121
  142.9 2.0 convolution_convert_fusion.2
  145.2 23.3 %reduce-scatter.2.cloned.1.call-done = bf16[160,2048]{1,0:T(8,128)(2,1)} async-done(((bf16[320,2048]{1,0:T(8,128)(2,1)}), bf16[160,2048]{1,0:T(8,128)(2,1)}) %reduce-scatter.2.cloned.1.call-update) | async-done | bytes 655376 | tf_op jit(solution)/shard_map/reduce_scatter | solution.py:122
  168.5 2.4 %fusion.37 = bf16[160,2048]{1,0:T(8,128)(2,1)} fusion(bf16[160,2048]{1,0:T(8,128)(2,1)} %reduce-scatter.2.cloned.1.call-done), kind=kLoop, calls=%fused_computation.32 | loop fusion | flops 3276800 | bytes 1310720 | tf_op jit(solution)/shard_map/convert_element_type | solution.py:125
  171.0 24.3 %all-gather.14.cloned.1.call-done = bf16[320,2048]{1,0:T(8,128)(2,1)} async-done(((bf16[160,2048]{1,0:T(8,128)(2,1)}), bf16[320,2048]{1,0:T(8,128)(2,1)}) %all-gather.14.cloned.1.call-update) | async-done | bytes 1310736 | tf_op jit(solution)/shard_map/all_gather | solution.py:126
  195.3 2.8 %convolution_convert_fusion.4 = bf16[320,512]{1,0:T(8,128)(2,1)S(1)} fusion(bf16[320,2048]{1,0:T(8,128)(2,1)} %all-gather.14.cloned.1.call-done, bf16[2048,512]{1,0:T(8,128)(2,1)} %param.24), kind=kOutput, calls=%fused_computation.35 | convolution fusion | flops 671252480 | bytes 3735552 | tf_op jit(solution)/shard_map/dot_general | solution.py:21
  198.1 8.5 %all_to_all.52 = bf16[2,160,512]{2,1,0:T(8,128)(2,1)S(1)} all-to-all(bf16[2,160,512]{2,1,0:T(8,128)(2,1)S(1)} %bitcast.56), channel_id=1, replica_groups=mesh['dp'=8,'mp'=2,'fsdp'=2] {'fsdp'}, dimensions={0} | all-to-all | bytes 655360 | tf_op jit(solution)/shard_map/all_to_all | solution.py:127
  206.6 0.8 copy.147
  207.5 0.8 reshape.228
  208.3 0.7 slice.46
  209.0 1.7 slice.45
  210.6 1.4 copy.141
  212.0 1.4 reshape.226
  213.4 1.6 fusion.58
  214.9 11.0 %all-reduce.5.cloned.1.call-done = bf16[160,1024]{1,0:T(8,128)(2,1)} async-done(((bf16[160,1024]{1,0:T(8,128)(2,1)}), bf16[160,1024]{1,0:T(8,128)(2,1)}) %all-reduce.5.cloned.1.call-update) | async-done | bytes 327696 | tf_op jit(solution)/shard_map/psum | solution.py:130
  225.9 1.2 fusion.55
  227.1 1.2 multiply_reduce_fusion.1
  228.6 0.9 copy.145
  (96 shorter events, 6.8 us)
Async XLA Ops:
  7.2 135.8 %copy-start = (bf16[512,2048]{1,0:T(8,128)(2,1)S(1)}, bf16[512,2048]{1,0:T(8,128)(2,1)}, u32[]{:S(2)}) copy-start(bf16[512,2048]{1,0:T(8,128)(2,1)} %param.23) | copy-start | bytes 6291460
  7.2 44.4 %all-gather.10.cloned.1.call-start = ((), (), s32[]{:S(2)}) async-start(), calls=%async_computation.6 | async-start | bytes 1572864 | tf_op jit(solution)/shard_map/all_gather | solution.py:55
  7.9 52.7 %all-gather.8.cloned.1.call-start = ((), (), s32[]{:S(2)}) async-start(), calls=%async_computation.5 | async-start | bytes 1572864 | tf_op jit(solution)/shard_map/all_gather | solution.py:54
  8.7 74.8 %all-gather.6.cloned.1.call-start = ((), (), s32[]{:S(2)}) async-start(), calls=%async_computation.4 | async-start | bytes 1572864 | tf_op jit(solution)/shard_map/all_gather | solution.py:56
  9.4 12.1 %copy-start.19 = (s32[32]{0:T(128)S(1)}, s32[32]{0:T(128)}, u32[]{:S(2)}) copy-start(s32[32]{0:T(128)} %param.15) | copy-start | bytes 388
  9.4 12.2 %copy-start.20 = (s32[32]{0:T(128)S(1)}, s32[32]{0:T(128)}, u32[]{:S(2)}) copy-start(s32[32]{0:T(128)} %param.18) | copy-start | bytes 388
  12.6 21.6 %all-to-all-start = ((bf16[320,16,32]{0,2,1:T(8,128)(2,1)}), bf16[320,16,32]{0,2,1:T(8,128)(2,1)S(1)}, u32[]{:S(2)}, u32[]{:S(2)}) async-start(bf16[320,16,32]{0,2,1:T(8,128)(2,1)} %all_to_all.38), calls=%async_computation | async-start | bytes 786432 | tf_op jit(solution)/shard_map/all_to_all | solution.py:47
  20.9 85.3 %all-gather.12.cloned.1.call-start = ((), (), s32[]{:S(2)}) async-start(), calls=%async_computation.7 | async-start | bytes 1572864 | tf_op jit(solution)/shard_map/all_gather | solution.py:112
  21.5 107.8 %all-reduce.3.cloned.1.call-start = ((), (), s32[]{:S(2)}) async-start(), calls=%async_computation.8 | async-start | bytes 786432 | tf_op jit(solution)/shard_map/psum | solution.py:114
  40.1 3.6 %copy-start.1 = (f32[16,5,64,32]{2,1,3,0:T(8,128)S(1)}, f32[16,5,64,32]{2,1,3,0:T(8,128)}, u32[]{:S(2)}) copy-start(f32[16,5,64,32]{2,1,3,0:T(8,128)} %reshape.233) | copy-start | bytes 1966084
  55.0 5.7 %copy-start.10 = (bf16[192,1024]{1,0:T(8,128)(2,1)S(1)}, bf16[192,1024]{1,0:T(8,128)(2,1)}, u32[]{:S(2)}) copy-start(bf16[192,1024]{1,0:T(8,128)(2,1)} %reshape.216) | copy-start | bytes 1179652
  67.5 4.3 %copy-start.2 = (bf16[32,64,8,64]{3,2,1,0:T(8,128)(2,1)S(1)}, bf16[32,64,8,64]{3,2,1,0:T(8,128)(2,1)}, u32[]{:S(2)}) copy-start(bf16[32,64,8,64]{3,2,1,0:T(8,128)(2,1)} %reshape.219) | copy-start | bytes 6291460
  68.0 8.5 %copy-start.6 = (f32[32,8,6,5]{2,3,1,0:T(8,128)}, f32[32,8,6,5]{2,3,1,0:T(8,128)S(1)}, u32[]{:S(2)}) copy-start(f32[32,8,6,5]{2,3,1,0:T(8,128)S(1)} %get-tuple-element.27) | copy-start | bytes 92164
  71.8 4.0 %copy-start.7 = (f32[32,8,6,32]{3,2,1,0:T(8,128)}, f32[32,8,6,32]{3,2,1,0:T(8,128)S(1)}, u32[]{:S(2)}) copy-start(f32[32,8,6,32]{3,2,1,0:T(8,128)S(1)} %get-tuple-element.29) | copy-start | bytes 589828
  74.2 1.0 copy-start.3
  86.9 1.0 copy-start.14
  87.9 4.0 %copy-start.12 = (bf16[160,512]{1,0:T(8,128)(2,1)}, bf16[160,512]{1,0:T(8,128)(2,1)S(1)}, u32[]{:S(2)}) copy-start(bf16[160,512]{1,0:T(8,128)(2,1)S(1)} %slice.42) | copy-start | bytes 491524
  88.9 3.0 %copy-start.16 = (f32[32,8,6]{2,1,0:T(8,128)}, f32[32,8,6]{2,1,0:T(8,128)S(1)}, u32[]{:S(2)}) copy-start(f32[32,8,6]{2,1,0:T(8,128)S(1)} %add_add_fusion) | copy-start | bytes 18436
  88.9 3.0 %copy-start.15 = (bf16[1184,512]{1,0:T(8,128)(2,1)S(1)}, bf16[1184,512]{1,0:T(8,128)(2,1)}, u32[]{:S(2)}) copy-start(bf16[1184,512]{1,0:T(8,128)(2,1)} %copy-done.14) | copy-start | bytes 3637252
  93.0 3.9 %copy-start.17 = (f32[32,8,6]{2,1,0:T(8,128)S(1)}, f32[32,8,6]{2,1,0:T(8,128)}, u32[]{:S(2)}) copy-start(f32[32,8,6]{2,1,0:T(8,128)} %copy-done.16) | copy-start | bytes 18436
  96.9 2.8 %copy-start.4 = (f32[32,8,6,64]{3,2,1,0:T(8,128)S(1)}, f32[32,8,6,64]{3,2,1,0:T(8,128)}, u32[]{:S(2)}) copy-start(f32[32,8,6,64]{3,2,1,0:T(8,128)} %copy-done.3) | copy-start | bytes 1179652
  96.9 3.5 %copy-start.5 = (bf16[32,64,8,64]{3,2,1,0:T(8,128)(2,1)S(1)}, bf16[32,64,8,64]{3,2,1,0:T(8,128)(2,1)}, u32[]{:S(2)}) copy-start(bf16[32,64,8,64]{3,2,1,0:T(8,128)(2,1)} %reshape.221) | copy-start | bytes 6291460
  96.9 3.7 %copy-start.21 = (f32[32,6,8,64]{3,1,2,0:T(8,128)S(1)}, f32[32,6,8,64]{3,1,2,0:T(8,128)}, u32[]{:S(2)}) copy-start(f32[32,6,8,64]{3,1,2,0:T(8,128)} %convolution_bitcast_fusion) | copy-start | bytes 1179652
  110.7 57.8 %reduce-scatter.2.cloned.1.call-start = ((), (), s32[]{:S(2)}) async-start(), calls=%async_computation.9 | async-start | bytes 1966080 | tf_op jit(solution)/shard_map/reduce_scatter | solution.py:122
  130.3 0.9 copy-start.8
  144.9 50.4 %all-gather.14.cloned.1.call-start = ((), (), s32[]{:S(2)}) async-start(), calls=%async_computation.10 | async-start | bytes 1966080 | tf_op jit(solution)/shard_map/all_gather | solution.py:126
  170.9 36.5 %copy-start.13 = (bf16[160,512]{1,0:T(8,128)(2,1)S(1)}, bf16[160,512]{1,0:T(8,128)(2,1)}, u32[]{:S(2)}) copy-start(bf16[160,512]{1,0:T(8,128)(2,1)} %copy-done.12) | copy-start | bytes 491524
  170.9 55.0 %all-reduce.5.cloned.1.call-start = ((), (), s32[]{:S(2)}) async-start(), calls=%async_computation.11 | async-start | bytes 655360 | tf_op jit(solution)/shard_map/psum | solution.py:130
  198.1 9.4 %copy-start.11 = (bf16[160,512]{1,0:T(8,128)(2,1)S(1)}, bf16[160,512]{1,0:T(8,128)(2,1)}, u32[]{:S(2)}) copy-start(bf16[160,512]{1,0:T(8,128)(2,1)} %slice.41) | copy-start | bytes 491524
  212.0 16.3 %copy-start.18 = (f32[1024]{0:T(1024)S(1)}, f32[1024]{0:T(1024)}, u32[]{:S(2)}) copy-start(f32[1024]{0:T(1024)} %param.25) | copy-start | bytes 12292
  225.9 2.4 %copy-start.9 = (bf16[160,1024]{1,0:T(8,128)(2,1)S(1)}, bf16[160,1024]{1,0:T(8,128)(2,1)}, u32[]{:S(2)}) copy-start(bf16[160,1024]{1,0:T(8,128)(2,1)} %all-reduce.5.cloned.1.call-done) | copy-start | bytes 983044
Sparse Core Ops, SparseCore 0:
  9.5 28.2 all-gather.9
  39.3 21.2 all-gather.7
  62.2 21.2 all-gather.5
  84.9 21.2 all-gather.11
  110.8 18.3 all-reduce.2
  145.0 23.4 reduce-scatter.1
  171.0 24.2 all-gather.13
  207.5 18.3 all-reduce.4
where the time goes:
time: 238 us; the launch traced here: 236 us
  waiting for transfers between devices  94 us (39%)
  local copies, waits for them, and re-layouts  56.7 us (24%)
  matrix products  29.4 us (12%)
  blocking collectives  17.6 us (7%)
  other arithmetic  15.2 us (6%)
  between operations  14.6 us (6%)
  starting transfers between devices  8.88 us (4%)
    all_gather x1, waiting for transfers between devices, shards(): lax.all_gather(hidden, 'fsdp', axis=0, tiled=True)  24.3 us
    reduce_scatter x1, waiting for transfers between devices, shards(): lax.psum_scatter(matmul(halves, w_up).astype(jnp.bfloat16), 'fsdp', scatt...  23.3 us
    psum x1, waiting for transfers between devices, shards(): lax.psum(attn_part.astype(jnp.bfloat16), 'mp').astype(jnp.float32)  18.5 us
    dot_general x6, matrix products, matmul(): return jnp.dot(left, right, preferred_element_type=jnp.float32)  15.5 us
    psum x1, waiting for transfers between devices, shards(): lax.psum(down_part.astype(jnp.bfloat16), 'mp').astype(jnp.float32)  11 us
    convert_element_type x5, local copies, waits for them, and re-layouts, shards(): hidden_state = inputs.astype(jnp.float32) + attn_out[:, :frames, :]  10.6 us
    all_to_all x1, blocking collectives, shards(): lax.all_to_all(h_norm, 'fsdp', split_axis=1, concat_axis=0, tiled=True)  9.13 us
    all_to_all x1, blocking collectives, shards(): lax.all_to_all(down_all.astype(jnp.bfloat16), 'fsdp', split_axis=0, conca...  8.51 us
  transfers between devices with their start and end apart: 9, of which 7 were waited for; matrix products, arithmetic and copies ran while one was open for 32% of the time, Pallas kernels for 0%

commit v1 on v0

--- a/solution.py
+++ b/solution.py
@@ -7,6 +7,11 @@
 GROUP = 4
 epsilon = 1e-05
 masked_score = -1e30
+
+
+def summed_here(x, axis):
+    blocks = lax.all_gather(x, axis)
+    return jnp.sum(blocks, axis=0)
 
 
 def normalize(values):
@@ -111,7 +116,7 @@
     attended = attended.astype(jnp.bfloat16).reshape(streams * (frames + 1), head_cols)
     attn_part = matmul(attended, lax.all_gather(w_out, "fsdp", axis=1, tiled=True))
     attn_out = (
-        lax.psum(attn_part.astype(jnp.bfloat16), "mp")
+        summed_here(attn_part.astype(jnp.bfloat16), "mp")
         .astype(jnp.float32)
         .reshape(streams, frames + 1, width)
     )

time: 238 us -> 221 us (0.929)
  waiting for transfers between devices: 94 us -> 76.6 us
    psum x1 -> x0, waiting for transfers between devices: 18.5 us -> none  [shards(): lax.psum(attn_part.astype(jnp.bfloat16), 'mp').astype(jnp.float32)]
    unnamed x46 -> x45, local copies, waits for them, and re-layouts: 6.48 us -> 6.39 us
  transfers between devices with their start and end apart: 9 -> 8, of which waited for: 7 -> 6; matrix products, arithmetic and copies ran while one was open for 32% -> 34% of each run, Pallas kernels for 0% -> 0%
where the time goes in v1:
time: 221 us; the launch traced here: 220 us
  waiting for transfers between devices  76.6 us (35%)
  local copies, waits for them, and re-layouts  55 us (25%)
  matrix products  28.6 us (13%)
  blocking collectives  19.7 us (9%)
  other arithmetic  16.5 us (7%)
  between operations  14.6 us (7%)
  starting transfers between devices  8.62 us (4%)
    all_gather x1, waiting for transfers between devices, shards(): lax.all_gather(hidden, 'fsdp', axis=0, tiled=True)  24.3 us
    reduce_scatter x1, waiting for transfers between devices, shards(): lax.psum_scatter(matmul(halves, w_up).astype(jnp.bfloat16), 'fsdp', scatt...  23.4 us
    dot_general x6, matrix products, matmul(): return jnp.dot(left, right, preferred_element_type=jnp.float32)  14.7 us
    psum x1, waiting for transfers between devices, shards(): lax.psum(down_part.astype(jnp.bfloat16), 'mp').astype(jnp.float32)  12.1 us
    convert_element_type x5, local copies, waits for them, and re-layouts, shards(): hidden_state = inputs.astype(jnp.float32) + attn_out[:, :frames, :]  10.7 us
    all_to_all x1, blocking collectives, shards(): lax.all_to_all(h_norm, 'fsdp', split_axis=1, concat_axis=0, tiled=True)  8.84 us
    all_to_all x1, blocking collectives, shards(): lax.all_to_all(down_all.astype(jnp.bfloat16), 'fsdp', split_axis=0, conca...  8.51 us
    all_to_all x1, starting transfers between devices, shards(): lax.all_to_all(flattened, ('dp', 'fsdp'), split_axis=1, concat_axis=0, ti...  8.34 us
  transfers between devices with their start and end apart: 8, of which 6 were waited for; matrix products, arithmetic and copies ran while one was open for 34% of the time, Pallas kernels for 0%

profile of v1, /device:TPU:0, one launch (start us, length us, event | category | flops | bytes accessed | tf_op | source)
XLA Modules:
  0.0 219.7 jit_solution(16970803745782834515)
XLA Ops:
  7.2 0.7 all-gather.11.cloned.1.call-update
  8.0 0.7 all-gather.9.cloned.1.call-update
  8.7 0.7 all-gather.7.cloned.1.call-update
  9.4 1.8 copy.119
  11.2 1.4 all_to_all.38
  12.5 8.3 %all-to-all-start = ((bf16[320,16,32]{0,2,1:T(8,128)(2,1)}), bf16[320,16,32]{0,2,1:T(8,128)(2,1)S(1)}, u32[]{:S(2)}, u32[]{:S(2)}) async-start(bf16[320,16,32]{0,2,1:T(8,128)(2,1)} %all_to_all.38), calls=%async_computation | async-start | bytes 786432 | tf_op jit(solution)/shard_map/all_to_all | solution.py:52
  21.6 6.2 %reshape.217 = bf16[32,64,8,64]{3,2,1,0:T(8,128)(2,1)} reshape(bf16[32,64,512]{2,1,0:T(8,128)(2,1)} %param.16) | data formatting | bytes 4194304 | tf_op jit(solution)/shard_map/reshape | solution.py:71
  27.8 6.2 %reshape.219 = bf16[32,64,8,64]{3,2,1,0:T(8,128)(2,1)} reshape(bf16[32,64,512]{2,1,0:T(8,128)(2,1)} %param.17) | data formatting | bytes 4194304 | tf_op jit(solution)/shard_map/reshape | solution.py:72
  34.2 1.7 reshape.230
  35.9 1.8 bitcast_reduce_fusion
  37.9 2.1 multiply_reduce_fusion
  40.1 3.6 %copy.120 = f32[32,5,16,64]{3,2,0,1:T(8,128)} copy(f32[32,5,16,64]{3,1,0,2:T(8,128)} %bitcast.54) | data formatting | bytes 1310720 | tf_op jit(solution)/shard_map/convert_element_type | solution.py:124
  43.7 1.9 copy.121
  45.7 1.8 reshape.226
  48.1 0.9 reshape.214
  49.0 1.7 reshape.227
  50.7 0.9 multiply_convert_fusion.3
  51.6 3.4 %convolution_convert_fusion = bf16[1184,512]{1,0:T(8,128)(2,1)S(1)} fusion(bf16[1024,512]{1,0:T(8,128)(2,1)} %all-gather.11.cloned.1.call-done, bf16[1024,1024]{1,0:T(8,128)(2,1)} %bitcast.63, bf16[160,1024]{1,0:T(8,128)(2,1)} %multiply_convert_fusion.3), kind=kOutput, calls=%fused_computation.4 | convolution fusion | flops 1246969856 | bytes 4685824 | tf_op jit(solution)/shard_map/dot_general | solution.py:26
  55.0 0.7 slice.41
  55.7 1.0 slice.40
  56.7 3.9 %all-gather.9.cloned.1.call-done = bf16[1024,512]{1,0:T(8,128)(2,1)} async-done(((bf16[512,512]{1,0:T(8,128)(2,1)}), bf16[1024,512]{1,0:T(8,128)(2,1)}) %all-gather.9.cloned.1.call-update) | async-done | bytes 1048592 | tf_op jit(solution)/shard_map/all_gather | solution.py:59
  60.6 1.6 convolution_convert_fusion.5
  62.5 1.1 reshape.218
  63.6 3.9 %reshape.216 = bf16[32,32,8,64]{3,2,1,0:T(8,128)(2,1)} reshape(bf16[1024,512]{1,0:T(8,128)(2,1)} %slice.40) | data formatting | bytes 2097152 | tf_op jit(solution)/shard_map/reshape | solution.py:69
  68.1 3.8 %fusion.62 = (f32[32,8,6]{2,1,0:T(8,128)S(1)}, f32[32,8,6,32]{3,2,1,0:T(8,128)S(1)}) fusion(bf16[32,32,8,64]{3,2,1,0:T(8,128)(2,1)} %reshape.216, bf16[32,6,8,64]{3,2,1,0:T(8,128)(2,1)S(1)} %reshape.215, pred[32,6,32]{2,1,0:T(8,128)(4,1)S(1)} %broadcast_and_fusion), kind=kOutput, calls=%fused_computation.93 | convolution fusion | flops 6437376 | bytes 1454080 | tf_op jit(solution)/shard_map/sqhd,skhd->shqk/dot_general | solution.py:82
  71.8 2.4 %fusion.63 = (f32[32,8,6]{2,1,0:T(8,128)S(1)}, f32[32,8,6,64]{3,2,1,0:T(8,128)S(1)}) fusion(bf16[32,64,8,64]{3,2,1,0:T(8,128)(2,1)S(1)} %copy-done.2, bf16[32,6,8,64]{3,2,1,0:T(8,128)(2,1)S(1)} %reshape.215, pred[32,64]{1,0:T(8,128)(4,1)S(1)} %iota_compare_fusion), kind=kOutput, calls=%fused_computation.94 | convolution fusion | flops 12876288 | bytes 2695168 | tf_op jit(solution)/shard_map/sqhd,skhd->shqk/dot_general | solution.py:85
  74.2 1.0 copy-done.3
  75.2 0.7 fusion.42
  75.9 0.7 fusion.41
  77.0 6.5 %all-gather.7.cloned.1.call-done = bf16[1024,512]{1,0:T(8,128)(2,1)} async-done(((bf16[512,512]{1,0:T(8,128)(2,1)}), bf16[1024,512]{1,0:T(8,128)(2,1)}) %all-gather.7.cloned.1.call-update) | async-done | bytes 1048592 | tf_op jit(solution)/shard_map/all_gather | solution.py:61
  83.5 3.4 %convolution_convert_fusion.1 = bf16[1184,512]{1,0:T(8,128)(2,1)S(1)} fusion(bf16[1024,512]{1,0:T(8,128)(2,1)} %all-gather.7.cloned.1.call-done, bf16[1024,1024]{1,0:T(8,128)(2,1)} %bitcast.64, bf16[160,1024]{1,0:T(8,128)(2,1)} %multiply_convert_fusion.3), kind=kOutput, calls=%fused_computation.5 | convolution fusion | flops 1246969856 | bytes 4685824 | tf_op jit(solution)/shard_map/dot_general | solution.py:26
  86.9 1.0 copy-done.13
  87.9 0.9 reshape.220
  88.9 3.0 %convolution_bitcast_fusion = f32[32,6,8,64]{3,1,2,0:T(8,128)} fusion(f32[32,8,6,5]{2,3,1,0:T(8,128)} %copy-done.6, bf16[32,5,8,64]{3,2,1,0:T(8,128)(2,1)} %reshape.220, f32[32,8,6]{2,1,0:T(8,128)S(1)} %add_add_fusion, f32[32,8,6]{2,1,0:T(8,128)S(1)} %maximum_maximum_fusion), kind=kOutput, calls=%fused_computation.23 | convolution fusion | flops 1006080 | bytes 600064 | tf_op jit(solution)/shard_map/shqk,skhd->sqhd/dot_general | solution.py:113
  92.0 1.0 slice.38
  93.0 3.9 %reshape.213 = bf16[32,32,8,64]{3,2,1,0:T(8,128)(2,1)} reshape(bf16[1024,512]{1,0:T(8,128)(2,1)} %slice.38) | data formatting | bytes 2097152 | tf_op jit(solution)/shard_map/reshape | solution.py:70
  97.0 2.7 %fusion.8 = f32[32,6,8,64]{3,1,2,0:T(8,128)S(1)} fusion(bf16[32,32,8,64]{3,2,1,0:T(8,128)(2,1)} %reshape.213, f32[32,8,6,32]{3,2,1,0:T(8,128)} %copy-done.7, f32[32,8,6]{2,1,0:T(8,128)S(1)} %copy-done.16, f32[32,8,6]{2,1,0:T(8,128)S(1)} %maximum_maximum_fusion), kind=kOutput, calls=%fused_computation.17 | convolution fusion | flops 6438912 | bytes 1650688 | tf_op jit(solution)/shard_map/shqk,skhd->sqhd/dot_general | solution.py:109
  99.7 0.7 copy-done.5
  100.7 1.5 fusion.38
  102.5 3.7 %all-gather.13.cloned.1.call-done = bf16[512,1024]{1,0:T(8,128)(2,1)} async-done(((bf16[512,512]{1,0:T(8,128)(2,1)}), bf16[512,1024]{1,0:T(8,128)(2,1)}) %all-gather.13.cloned.1.call-update) | async-done | bytes 1048592 | tf_op jit(solution)/shard_map/all_gather | solution.py:117
  106.2 1.6 convolution_convert_fusion.3
  107.8 2.4 %all-gather = bf16[384,1024]{1,0:T(8,128)(2,1)S(1)} all-gather(bf16[192,1024]{1,0:T(8,128)(2,1)S(1)} %convolution_convert_fusion.3), channel_id=2, replica_groups=mesh['dp'=8,'mp'=2,'fsdp'=2] {'mp'}, dimensions={0}, use_global_device_ids=true | all-gather | bytes 1179648 | tf_op jit(solution)/shard_map/all_gather | solution.py:13
  110.2 1.0 reduce_sum.108
  111.2 2.1 reshape.228
  113.3 1.7 fusion.60
  115.5 1.0 all_to_all.40
  116.5 1.0 copy.142
  117.5 8.8 %all_to_all.51 = bf16[160,2,512]{2,0,1:T(8,128)(2,1)S(1)} all-to-all(bf16[160,2,512]{2,0,1:T(8,128)(2,1)S(1)} %copy.142), channel_id=1, replica_groups=mesh['dp'=8,'mp'=2,'fsdp'=2] {'fsdp'}, dimensions={1} | all-to-all | bytes 655360 | tf_op jit(solution)/shard_map/all_to_all | solution.py:126
  126.4 2.0 convolution_convert_fusion.2
  128.4 23.4 %reduce-scatter.2.cloned.1.call-done = bf16[160,2048]{1,0:T(8,128)(2,1)} async-done(((bf16[320,2048]{1,0:T(8,128)(2,1)}), bf16[160,2048]{1,0:T(8,128)(2,1)}) %reduce-scatter.2.cloned.1.call-update) | async-done | bytes 655376 | tf_op jit(solution)/shard_map/reduce_scatter | solution.py:127
  151.8 2.4 %fusion.37 = bf16[160,2048]{1,0:T(8,128)(2,1)} fusion(bf16[160,2048]{1,0:T(8,128)(2,1)} %reduce-scatter.2.cloned.1.call-done), kind=kLoop, calls=%fused_computation.32 | loop fusion | flops 3276800 | bytes 1310720 | tf_op jit(solution)/shard_map/convert_element_type | solution.py:130
  154.2 24.3 %all-gather.15.cloned.1.call-done = bf16[320,2048]{1,0:T(8,128)(2,1)} async-done(((bf16[160,2048]{1,0:T(8,128)(2,1)}), bf16[320,2048]{1,0:T(8,128)(2,1)}) %all-gather.15.cloned.1.call-update) | async-done | bytes 1310736 | tf_op jit(solution)/shard_map/all_gather | solution.py:131
  178.6 2.8 %convolution_convert_fusion.4 = bf16[320,512]{1,0:T(8,128)(2,1)S(1)} fusion(bf16[320,2048]{1,0:T(8,128)(2,1)} %all-gather.15.cloned.1.call-done, bf16[2048,512]{1,0:T(8,128)(2,1)} %param.24), kind=kOutput, calls=%fused_computation.35 | convolution fusion | flops 671252480 | bytes 3735552 | tf_op jit(solution)/shard_map/dot_general | solution.py:26
  181.4 8.5 %all_to_all.52 = bf16[2,160,512]{2,1,0:T(8,128)(2,1)S(1)} all-to-all(bf16[2,160,512]{2,1,0:T(8,128)(2,1)S(1)} %bitcast.61), channel_id=1, replica_groups=mesh['dp'=8,'mp'=2,'fsdp'=2] {'fsdp'}, dimensions={0} | all-to-all | bytes 655360 | tf_op jit(solution)/shard_map/all_to_all | solution.py:132
  189.9 0.8 copy.148
  190.7 1.4 copy.140
  192.3 1.3 reshape.222
  193.7 1.4 fusion.56
  195.7 0.7 slice.46
  196.4 0.7 slice.45
  197.1 12.1 %all-reduce.2.cloned.1.call-done = bf16[160,1024]{1,0:T(8,128)(2,1)} async-done(((bf16[160,1024]{1,0:T(8,128)(2,1)}), bf16[160,1024]{1,0:T(8,128)(2,1)}) %all-reduce.2.cloned.1.call-update) | async-done | bytes 327696 | tf_op jit(solution)/shard_map/psum | solution.py:135
  209.2 1.2 fusion.55
  210.4 1.2 multiply_reduce_fusion.1
  211.9 0.9 copy.144
  (92 shorter events, 5.8 us)
Async XLA Ops:
  7.2 119.2 %copy-start = (bf16[512,2048]{1,0:T(8,128)(2,1)S(1)}, bf16[512,2048]{1,0:T(8,128)(2,1)}, u32[]{:S(2)}) copy-start(bf16[512,2048]{1,0:T(8,128)(2,1)} %param.23) | copy-start | bytes 6291460
  7.2 44.4 %all-gather.11.cloned.1.call-start = ((), (), s32[]{:S(2)}) async-start(), calls=%async_computation.6 | async-start | bytes 1572864 | tf_op jit(solution)/shard_map/all_gather | solution.py:60
  7.9 52.7 %all-gather.9.cloned.1.call-start = ((), (), s32[]{:S(2)}) async-start(), calls=%async_computation.5 | async-start | bytes 1572864 | tf_op jit(solution)/shard_map/all_gather | solution.py:59
  8.7 74.8 %all-gather.7.cloned.1.call-start = ((), (), s32[]{:S(2)}) async-start(), calls=%async_computation.4 | async-start | bytes 1572864 | tf_op jit(solution)/shard_map/all_gather | solution.py:61
  9.4 12.1 %copy-start.18 = (s32[32]{0:T(128)S(1)}, s32[32]{0:T(128)}, u32[]{:S(2)}) copy-start(s32[32]{0:T(128)} %param.15) | copy-start | bytes 388
  9.4 12.2 %copy-start.19 = (s32[32]{0:T(128)S(1)}, s32[32]{0:T(128)}, u32[]{:S(2)}) copy-start(s32[32]{0:T(128)} %param.18) | copy-start | bytes 388
  12.5 21.6 %all-to-all-start = ((bf16[320,16,32]{0,2,1:T(8,128)(2,1)}), bf16[320,16,32]{0,2,1:T(8,128)(2,1)S(1)}, u32[]{:S(2)}, u32[]{:S(2)}) async-start(bf16[320,16,32]{0,2,1:T(8,128)(2,1)} %all_to_all.38), calls=%async_computation | async-start | bytes 786432 | tf_op jit(solution)/shard_map/all_to_all | solution.py:52
  20.9 85.3 %all-gather.13.cloned.1.call-start = ((), (), s32[]{:S(2)}) async-start(), calls=%async_computation.7 | async-start | bytes 1572864 | tf_op jit(solution)/shard_map/all_gather | solution.py:117
  21.5 130.3 %reduce-scatter.2.cloned.1.call-start = ((), (), s32[]{:S(2)}) async-start(), calls=%async_computation.8 | async-start | bytes 1966080 | tf_op jit(solution)/shard_map/reduce_scatter | solution.py:127
  40.1 3.6 %copy-start.1 = (f32[16,5,64,32]{2,1,3,0:T(8,128)S(1)}, f32[16,5,64,32]{2,1,3,0:T(8,128)}, u32[]{:S(2)}) copy-start(f32[16,5,64,32]{2,1,3,0:T(8,128)} %reshape.230) | copy-start | bytes 1966084
  55.0 5.7 %copy-start.9 = (bf16[192,1024]{1,0:T(8,128)(2,1)S(1)}, bf16[192,1024]{1,0:T(8,128)(2,1)}, u32[]{:S(2)}) copy-start(bf16[192,1024]{1,0:T(8,128)(2,1)} %reshape.214) | copy-start | bytes 1179652
  67.5 4.3 %copy-start.2 = (bf16[32,64,8,64]{3,2,1,0:T(8,128)(2,1)S(1)}, bf16[32,64,8,64]{3,2,1,0:T(8,128)(2,1)}, u32[]{:S(2)}) copy-start(bf16[32,64,8,64]{3,2,1,0:T(8,128)(2,1)} %reshape.217) | copy-start | bytes 6291460
  68.1 8.5 %copy-start.6 = (f32[32,8,6,5]{2,3,1,0:T(8,128)}, f32[32,8,6,5]{2,3,1,0:T(8,128)S(1)}, u32[]{:S(2)}) copy-start(f32[32,8,6,5]{2,3,1,0:T(8,128)S(1)} %get-tuple-element.27) | copy-start | bytes 92164
  71.8 4.0 %copy-start.7 = (f32[32,8,6,32]{3,2,1,0:T(8,128)}, f32[32,8,6,32]{3,2,1,0:T(8,128)S(1)}, u32[]{:S(2)}) copy-start(f32[32,8,6,32]{3,2,1,0:T(8,128)S(1)} %get-tuple-element.29) | copy-start | bytes 589828
  74.2 1.0 copy-start.3
  86.9 1.0 copy-start.13
  87.9 4.0 %copy-start.11 = (bf16[160,512]{1,0:T(8,128)(2,1)}, bf16[160,512]{1,0:T(8,128)(2,1)S(1)}, u32[]{:S(2)}) copy-start(bf16[160,512]{1,0:T(8,128)(2,1)S(1)} %slice.42) | copy-start | bytes 491524
  88.9 3.1 %copy-start.15 = (f32[32,8,6]{2,1,0:T(8,128)}, f32[32,8,6]{2,1,0:T(8,128)S(1)}, u32[]{:S(2)}) copy-start(f32[32,8,6]{2,1,0:T(8,128)S(1)} %add_add_fusion) | copy-start | bytes 18436
  88.9 3.1 %copy-start.14 = (bf16[1184,512]{1,0:T(8,128)(2,1)S(1)}, bf16[1184,512]{1,0:T(8,128)(2,1)}, u32[]{:S(2)}) copy-start(bf16[1184,512]{1,0:T(8,128)(2,1)} %copy-done.13) | copy-start | bytes 3637252
  93.0 3.9 %copy-start.16 = (f32[32,8,6]{2,1,0:T(8,128)S(1)}, f32[32,8,6]{2,1,0:T(8,128)}, u32[]{:S(2)}) copy-start(f32[32,8,6]{2,1,0:T(8,128)} %copy-done.15) | copy-start | bytes 18436
  97.0 2.8 %copy-start.4 = (f32[32,8,6,64]{3,2,1,0:T(8,128)S(1)}, f32[32,8,6,64]{3,2,1,0:T(8,128)}, u32[]{:S(2)}) copy-start(f32[32,8,6,64]{3,2,1,0:T(8,128)} %copy-done.3) | copy-start | bytes 1179652
  97.0 3.5 %copy-start.5 = (bf16[32,64,8,64]{3,2,1,0:T(8,128)(2,1)S(1)}, bf16[32,64,8,64]{3,2,1,0:T(8,128)(2,1)}, u32[]{:S(2)}) copy-start(bf16[32,64,8,64]{3,2,1,0:T(8,128)(2,1)} %reshape.219) | copy-start | bytes 6291460
  97.0 3.7 %copy-start.20 = (f32[32,6,8,64]{3,1,2,0:T(8,128)S(1)}, f32[32,6,8,64]{3,1,2,0:T(8,128)}, u32[]{:S(2)}) copy-start(f32[32,6,8,64]{3,1,2,0:T(8,128)} %convolution_bitcast_fusion) | copy-start | bytes 1179652
  128.4 50.2 %all-gather.15.cloned.1.call-start = ((), (), s32[]{:S(2)}) async-start(), calls=%async_computation.9 | async-start | bytes 1966080 | tf_op jit(solution)/shard_map/all_gather | solution.py:131
  154.2 55.0 %all-reduce.2.cloned.1.call-start = ((), (), s32[]{:S(2)}) async-start(), calls=%async_computation.10 | async-start | bytes 655360 | tf_op jit(solution)/shard_map/psum | solution.py:135
  181.4 10.7 %copy-start.12 = (bf16[160,512]{1,0:T(8,128)(2,1)S(1)}, bf16[160,512]{1,0:T(8,128)(2,1)}, u32[]{:S(2)}) copy-start(bf16[160,512]{1,0:T(8,128)(2,1)} %copy-done.11) | copy-start | bytes 491524
  181.4 10.8 %copy-start.10 = (bf16[160,512]{1,0:T(8,128)(2,1)S(1)}, bf16[160,512]{1,0:T(8,128)(2,1)}, u32[]{:S(2)}) copy-start(bf16[160,512]{1,0:T(8,128)(2,1)} %slice.41) | copy-start | bytes 491524
  192.3 19.3 %copy-start.17 = (f32[1024]{0:T(1024)S(1)}, f32[1024]{0:T(1024)}, u32[]{:S(2)}) copy-start(f32[1024]{0:T(1024)} %param.25) | copy-start | bytes 12292
  209.2 2.4 %copy-start.8 = (bf16[160,1024]{1,0:T(8,128)(2,1)S(1)}, bf16[160,1024]{1,0:T(8,128)(2,1)}, u32[]{:S(2)}) copy-start(bf16[160,1024]{1,0:T(8,128)(2,1)} %all-reduce.2.cloned.1.call-done) | copy-start | bytes 983044
Sparse Core Ops, SparseCore 0:
  9.5 28.2 all-gather.10
  39.3 21.2 all-gather.8
  62.2 21.2 all-gather.6
  84.9 21.2 all-gather.12
  128.5 23.2 reduce-scatter.1
  154.3 24.2 all-gather.14
  190.8 18.3 all-reduce.1
